TPU v7x, 32 devices: a whole 2x2x4 slice. The times are simulated.
32 devices in a mesh: cond: 2 (over x), gx: 4 (over y, core), yz: 4 (over z).
Axes of the slice: x: 2, y: 2, z: 4, core: 2. Of those that a mesh axis runs over, the one named last changes fastest.
Arguments:
- adjoint: float32 [2, 5, 32, 64, 256], P('cond', None, 'gx', 'yz'), may hold values from -6 to 6
- objective_gradient: float32 [2, 5, 32, 64, 256], P('cond', None, 'gx', 'yz'), may hold values from -6 to 6
- diagonal: float32 [32, 64, 256], P('gx', 'yz'), may hold values from 4 to 12
- flux_blocks: float32 [2, 6, 5, 5], P('cond'), may hold values from -1 to 1
- flux_sensitivity: bfloat16 [2, 5, 32, 64, 256], P('cond', None, 'gx', 'yz'), may hold values from -6 to 6
- surface_mask: int32 [32, 64, 256], P('gx', 'yz'), may hold values 0 or 1
- patch_band_slot: int32 [32, 64], P('gx', 'yz'), may hold values from 0 to 62
- design_basis: float32 [256, 128], replicated, may hold values from -0.046875 to 0.046875
- condition_weights: int32 [2], replicated, may hold values from 1 to 999, as said below
Outputs:
- smoothed: float32 [2, 5, 32, 64, 256], P('cond', None, 'gx', 'yz')
- residual: float32 [2, 5, 32, 64, 256], P('cond', None, 'gx', 'yz')
- design_gradient: float32 [4096], P(('gx', 'yz'))
Inputs may be any that keep to these rules, and one draw needn't show every extreme that they name: `condition_weights`: positive integer weights; one condition has weight 999.
All inputs are finite; a program needn't handle non-finite values. No bound on the sum of `surface_mask` on one device may be relied on, other than what follows from the above.
Results may differ from a plain program's by a relative error of at most 0.0003.
Values sent between devices are 32-bit elements; how exact they have to be, the bound alone decides.
A program may use at most 64 MiB of HBM per device.

v0:
```python
import jax
import jax.numpy as jnp
from jax import lax
from jax.sharding import PartitionSpec as P

NDES = 4096
relaxation = 0.8
neighbour_starts = ((2, 1, 1), (0, 1, 1), (1, 2, 1), (1, 0, 1), (1, 1, 2), (1, 1, 0))


def with_halo(block, sides, width):
    for axis, dim in sides:
        count = lax.axis_size(axis)
        forward = [(i, i + 1) for i in range(count - 1)]
        backward = [(target, source) for source, target in forward]
        low = lax.ppermute(
            lax.slice_in_dim(block, block.shape[dim] - width, None, axis=dim), axis, forward
        )
        high = lax.ppermute(lax.slice_in_dim(block, 0, width, axis=dim), axis, backward)
        block = jnp.concatenate([low, block, high], axis=dim)
    return block


def apply_operator(padded_field, diagonal, blocks):
    size_x = padded_field.shape[1] - 2
    size_y = padded_field.shape[2] - 2
    size_z = padded_field.shape[3] - 2
    result = diagonal * padded_field[:, 1:-1, 1:-1, 1:-1]
    for direction in range(6):
        start_x, start_y, start_z = neighbour_starts[direction]
        shifted = padded_field[
            :, start_x : start_x + size_x, start_y : start_y + size_y, start_z : start_z + size_z
        ]
        result = result - jnp.einsum(
            "ec,exyz->cxyz", blocks[direction], shifted, precision=lax.Precision.HIGHEST
        )
    return result


def spread_bands(slot_lookup):
    halfway = slot_lookup.shape[1] // 2
    first_half = jnp.pad(slot_lookup[:, :halfway], ((0, 1), (0, 0)))
    second_half = jnp.pad(slot_lookup[:, halfway:], ((1, 0), (0, 0)))
    return (first_half + second_half).reshape(-1)


def pad_third(values):
    return jnp.pad(values, ((0, 0), (0, 0), (0, 0), (1, 1)))


def local(
    adjoint,
    objective_gradient,
    diagonal,
    flux_blocks,
    flux_sensitivity,
    surface_mask,
    patch_band_slot,
    design_basis,
    condition_weights,
):
    blocks = flux_blocks[0]
    source = objective_gradient[0]
    start_field = adjoint[0]

    def operate(values):
        haloed = with_halo(values, (("gx", 1), ("yz", 2)), 1)
        return apply_operator(pad_third(haloed), diagonal, blocks)

    relaxed = start_field + relaxation * (source - operate(start_field)) / diagonal
    smoothed = relaxed + relaxation * (source - operate(relaxed)) / diagonal
    residual = source - operate(smoothed)
    surface = surface_mask.astype(jnp.float32) * jnp.sum(
        smoothed * flux_sensitivity[0].astype(jnp.float32), axis=0
    )
    projected_gradient = jnp.dot(
        surface.reshape(-1, surface.shape[-1]),
        design_basis,
        precision=lax.Precision.HIGHEST,
        preferred_element_type=jnp.float32,
    )
    slot_count = 2 * NDES // design_basis.shape[1] - 1
    onehot = (jnp.arange(slot_count)[:, None] == patch_band_slot.reshape(1, -1)).astype(jnp.float32)
    slot_lookup = jnp.dot(
        onehot,
        projected_gradient,
        precision=lax.Precision.HIGHEST,
        preferred_element_type=jnp.float32,
    )
    gradient = spread_bands(slot_lookup)
    weights_float = condition_weights.astype(jnp.float32)
    picked = jnp.arange(weights_float.shape[0]) == lax.axis_index("cond")
    local_portion = jnp.sum(jnp.where(picked, weights_float, 0.0)) / jnp.sum(weights_float)
    summed = lax.psum(local_portion * gradient, ("cond", "gx", "yz"))
    pieces = NDES // lax.axis_size(("gx", "yz"))
    design_gradient = lax.dynamic_slice_in_dim(
        summed, lax.axis_index(("gx", "yz")) * pieces, pieces, 0
    )
    return (smoothed[None], residual[None], design_gradient)


def solution(mesh):
    placed = (
        P("cond", None, "gx", "yz", None),
        P("cond", None, "gx", "yz", None),
        P("gx", "yz", None),
        P("cond", None, None, None),
        P("cond", None, "gx", "yz", None),
        P("gx", "yz", None),
        P("gx", "yz"),
        P(),
        P(),
    )
    return jax.shard_map(
        local,
        mesh=mesh,
        in_specs=placed,
        out_specs=(
            P("cond", None, "gx", "yz", None),
            P("cond", None, "gx", "yz", None),
            P(("gx", "yz")),
        ),
        check_vma=False,
    )
```

profile of v0, /device:TPU:12, one launch (start us, length us, event | category | flops | bytes accessed | tf_op | source)
XLA Modules:
  0.0 115.4 jit_solution(11190379338171602337)
XLA Ops:
  0.7 1.5 %copy.88 = f32[1,5,8,16,256]{4,1,3,2,0:T(8,128)S(1)} copy(f32[1,5,8,16,256]{4,3,2,1,0:T(8,128)} %param.9) | data formatting | bytes 1310720 | tf_op args[0]
  2.2 1.9 %collective-permute-start = (f32[5,1,16,256]{3,0,2,1:T(8,128)S(1)}, f32[5,1,16,256]{3,0,2,1:T(8,128)S(1)}, u32[]{:S(2)}, u32[]{:S(2)}) collective-permute-start(f32[5,1,16,256]{3,0,2,1:T(8,128)S(1)} %get-tuple-element.19), channel_id=1, source_target_pairs={{4,0},{8,4},{12,8},{5,1},{9,5},{13,9},{6,2},{10,6},{14,10},{7,3},{... | collective-permute-start | bytes 245768 | tf_op jit(solution)/shard_map/ppermute | solution.py:19
  4.1 2.4 %collective-permute-start.1 = (f32[5,1,16,256]{3,0,2,1:T(8,128)S(1)}, f32[5,1,16,256]{3,0,2,1:T(8,128)S(1)}, u32[]{:S(2)}, u32[]{:S(2)}) collective-permute-start(f32[5,1,16,256]{3,0,2,1:T(8,128)S(1)} %get-tuple-element.18), channel_id=1, source_target_pairs={{0,4},{4,8},{8,12},{1,5},{5,9},{9,13},{2,6},{6,10},{10,14},{3,7},{... | collective-permute-start | bytes 245768 | tf_op jit(solution)/shard_map/ppermute | solution.py:16
  6.6 0.2 fusion.157
  6.8 0.1 copy.82
  7.7 2.8 %collective-permute-done.1 = f32[5,1,16,256]{3,0,2,1:T(8,128)S(1)} collective-permute-done((f32[5,1,16,256]{3,0,2,1:T(8,128)S(1)}, f32[5,1,16,256]{3,0,2,1:T(8,128)S(1)}, u32[]{:S(2)}, u32[]{:S(2)}) %collective-permute-start.1) | collective-permute-done | bytes 81952 | tf_op jit(solution)/shard_map/ppermute | solution.py:16
  10.4 2.4 %collective-permute-start.2 = (f32[5,10,1,256]{3,0,2,1:T(8,128)S(1)}, f32[5,10,1,256]{3,0,2,1:T(8,128)S(1)}, u32[]{:S(2)}, u32[]{:S(2)}) collective-permute-start(f32[5,10,1,256]{3,0,2,1:T(8,128)S(1)} %get-tuple-element.13), channel_id=1, source_target_pairs={{1,0},{2,1},{3,2},{5,4},{6,5},{7,6},{9,8},{10,9},{11,10},{13,12},{... | collective-permute-start | bytes 153608 | tf_op jit(solution)/shard_map/ppermute | solution.py:19
  12.8 3.5 %collective-permute-start.3 = (f32[5,10,1,256]{3,0,2,1:T(8,128)S(1)}, f32[5,10,1,256]{3,0,2,1:T(8,128)S(1)}, u32[]{:S(2)}, u32[]{:S(2)}) collective-permute-start(f32[5,10,1,256]{3,0,2,1:T(8,128)S(1)} %get-tuple-element.12), channel_id=1, source_target_pairs={{0,1},{1,2},{2,3},{4,5},{5,6},{6,7},{8,9},{9,10},{10,11},{12,13},{... | collective-permute-start | bytes 153608 | tf_op jit(solution)/shard_map/ppermute | solution.py:16
  16.3 1.1 convolution_bitcast_fusion.4
  17.4 1.8 %collective-permute-done.3 = f32[5,10,1,256]{3,0,2,1:T(8,128)S(1)} collective-permute-done((f32[5,10,1,256]{3,0,2,1:T(8,128)S(1)}, f32[5,10,1,256]{3,0,2,1:T(8,128)S(1)}, u32[]{:S(2)}, u32[]{:S(2)}) %collective-permute-start.3) | collective-permute-done | bytes 51232 | tf_op jit(solution)/shard_map/ppermute | solution.py:16
  19.1 0.6 select_maximum_fusion.8
  19.8 1.0 convolution_bitcast_fusion.10
  20.9 1.2 %convolution_bitcast_fusion.11 = f32[5,8,16,256]{3,0,2,1:T(8,128)S(1)} fusion(f32[5,10,18,258]{3,0,2,1:T(8,128)S(1)} %select_maximum_fusion.8, f32[1,1,5,5]{3,2,1,0:T(8,128)S(1)} %copy.81), kind=kOutput, calls=%fused_computation.86 | convolution fusion | flops 9830400 | bytes 1708032 | tf_op jit(solution)/shard_map/ec,exyz->cxyz/dot_general | solution.py:34
  22.1 1.1 fusion.61
  23.2 1.1 fusion.64
  24.3 2.0 %fusion.94 = f32[5,8,16,256]{3,0,2,1:T(8,128)S(1)} fusion(f32[5,8,16,256]{3,0,2,1:T(8,128)S(1)} %bitcast.184, f32[5,8,16,256]{3,0,2,1:T(8,128)S(1)} %convolution_bitcast_fusion.10, f32[5,8,16,256]{3,0,2,1:T(8,128)S(1)} %convolution_bitcast_fusion.11, f32[5,8,16,256]{3,0,2,1:T(8,128)S(1)} %fusion.61, f32[5,8,16,256]{3,0,2,1:T(8,128)S(1)} %fusion.64, ...), kind=kOutput, calls=%fused_computation.108 | convolution fusion | flops 11816960 | bytes 5455972 | tf_op jit(solution)/shard_map/ec,exyz->cxyz/dot_general | solution.py:34
  26.3 1.9 %collective-permute-start.4 = (f32[5,1,16,256]{3,0,2,1:T(8,128)S(1)}, f32[5,1,16,256]{3,0,2,1:T(8,128)S(1)}, u32[]{:S(2)}, u32[]{:S(2)}) collective-permute-start(f32[5,1,16,256]{3,0,2,1:T(8,128)S(1)} %get-tuple-element.17), channel_id=1, source_target_pairs={{4,0},{8,4},{12,8},{5,1},{9,5},{13,9},{6,2},{10,6},{14,10},{7,3},{... | collective-permute-start | bytes 245768 | tf_op jit(solution)/shard_map/ppermute | solution.py:19
  28.3 2.4 %collective-permute-start.5 = (f32[5,1,16,256]{3,0,2,1:T(8,128)S(1)}, f32[5,1,16,256]{3,0,2,1:T(8,128)S(1)}, u32[]{:S(2)}, u32[]{:S(2)}) collective-permute-start(f32[5,1,16,256]{3,0,2,1:T(8,128)S(1)} %get-tuple-element.16), channel_id=1, source_target_pairs={{0,4},{4,8},{8,12},{1,5},{5,9},{9,13},{2,6},{6,10},{10,14},{3,7},{... | collective-permute-start | bytes 245768 | tf_op jit(solution)/shard_map/ppermute | solution.py:16
  30.7 0.6 convert_reduce_fusion
  32.7 1.9 %collective-permute-done.5 = f32[5,1,16,256]{3,0,2,1:T(8,128)S(1)} collective-permute-done((f32[5,1,16,256]{3,0,2,1:T(8,128)S(1)}, f32[5,1,16,256]{3,0,2,1:T(8,128)S(1)}, u32[]{:S(2)}, u32[]{:S(2)}) %collective-permute-start.5) | collective-permute-done | bytes 81952 | tf_op jit(solution)/shard_map/ppermute | solution.py:16
  34.6 1.9 %collective-permute-start.6 = (f32[5,10,1,256]{3,0,2,1:T(8,128)S(1)}, f32[5,10,1,256]{3,0,2,1:T(8,128)S(1)}, u32[]{:S(2)}, u32[]{:S(2)}) collective-permute-start(f32[5,10,1,256]{3,0,2,1:T(8,128)S(1)} %get-tuple-element.11), channel_id=1, source_target_pairs={{1,0},{2,1},{3,2},{5,4},{6,5},{7,6},{9,8},{10,9},{11,10},{13,12},{... | collective-permute-start | bytes 153608 | tf_op jit(solution)/shard_map/ppermute | solution.py:19
  36.5 4.1 %collective-permute-start.7 = (f32[5,10,1,256]{3,0,2,1:T(8,128)S(1)}, f32[5,10,1,256]{3,0,2,1:T(8,128)S(1)}, u32[]{:S(2)}, u32[]{:S(2)}) collective-permute-start(f32[5,10,1,256]{3,0,2,1:T(8,128)S(1)} %get-tuple-element.10), channel_id=1, source_target_pairs={{0,1},{1,2},{2,3},{4,5},{5,6},{6,7},{8,9},{9,10},{10,11},{12,13},{... | collective-permute-start | bytes 153608 | tf_op jit(solution)/shard_map/ppermute | solution.py:16
  40.6 1.1 convolution_bitcast_fusion.2
  41.7 1.1 collective-permute-done.7
  42.8 0.6 select_maximum_fusion.4
  43.5 1.0 convolution_bitcast_fusion.8
  44.5 1.2 %convolution_bitcast_fusion.9 = f32[5,8,16,256]{3,0,2,1:T(8,128)S(1)} fusion(f32[5,10,18,258]{3,0,2,1:T(8,128)S(1)} %select_maximum_fusion.4, f32[1,1,5,5]{3,2,1,0:T(8,128)S(1)} %copy.81), kind=kOutput, calls=%fused_computation.84 | convolution fusion | flops 9830400 | bytes 1708032 | tf_op jit(solution)/shard_map/ec,exyz->cxyz/dot_general | solution.py:34
  45.8 1.1 fusion.55
  46.9 1.1 fusion.58
  47.9 2.2 %fusion.119 = (f32[8,16,256]{2,1,0:T(8,128)S(1)}, f32[5,8,16,256]{3,0,2,1:T(8,128)S(1)}) fusion(bf16[1,5,8,16,256]{4,3,2,1,0:T(8,128)(2,1)S(1)} %copy-done.3, f32[5,8,16,256]{3,0,2,1:T(8,128)S(1)} %fusion.94, f32[5,8,16,256]{3,0,2,1:T(8,128)S(1)} %convolution_bitcast_fusion.8, f32[5,8,16,256]{3,0,2,1:T(8,128)S(1)} %convolution_bitcast_fusion.9, ...), kind=kOutput, calls=%fused_computation.134 | convolution fusion | flops 12275712 | bytes 5914724 | tf_op jit(solution)/shard_map/ec,exyz->cxyz/dot_general | solution.py:34
  50.2 1.0 copy.39
  51.2 1.9 %collective-permute-start.8 = (f32[5,1,16,256]{3,0,2,1:T(8,128)S(1)}, f32[5,1,16,256]{3,0,2,1:T(8,128)S(1)}, u32[]{:S(2)}, u32[]{:S(2)}) collective-permute-start(f32[5,1,16,256]{3,0,2,1:T(8,128)S(1)} %get-tuple-element.15), channel_id=1, source_target_pairs={{4,0},{8,4},{12,8},{5,1},{9,5},{13,9},{6,2},{10,6},{14,10},{7,3},{... | collective-permute-start | bytes 245768 | tf_op jit(solution)/shard_map/ppermute | solution.py:19
  53.1 2.4 %collective-permute-start.9 = (f32[5,1,16,256]{3,0,2,1:T(8,128)S(1)}, f32[5,1,16,256]{3,0,2,1:T(8,128)S(1)}, u32[]{:S(2)}, u32[]{:S(2)}) collective-permute-start(f32[5,1,16,256]{3,0,2,1:T(8,128)S(1)} %get-tuple-element.14), channel_id=1, source_target_pairs={{0,4},{4,8},{8,12},{1,5},{5,9},{9,13},{2,6},{6,10},{10,14},{3,7},{... | collective-permute-start | bytes 245768 | tf_op jit(solution)/shard_map/ppermute | solution.py:16
  55.6 0.3 fusion.158
  55.8 0.2 fusion.120
  56.2 41.7 %psum.7 = f32[4096]{0:T(1024)S(1)} all-reduce(f32[4096]{0:T(1024)S(1)} %mul.57), channel_id=1, replica_groups=mesh['cond'=2,'gx'=4,'yz'=4] {'cond','gx','yz'}, use_global_device_ids=true, to_apply=%region_3.4 | all-reduce | flops 4096 | bytes 32768 | tf_op jit(solution)/shard_map/psum | solution.py:94
  97.9 0.6 dynamic_slice.3
  98.5 2.4 %collective-permute-start.10 = (f32[5,10,1,256]{3,0,2,1:T(8,128)S(1)}, f32[5,10,1,256]{3,0,2,1:T(8,128)S(1)}, u32[]{:S(2)}, u32[]{:S(2)}) collective-permute-start(f32[5,10,1,256]{3,0,2,1:T(8,128)S(1)} %get-tuple-element.9), channel_id=1, source_target_pairs={{1,0},{2,1},{3,2},{5,4},{6,5},{7,6},{9,8},{10,9},{11,10},{13,12},{... | collective-permute-start | bytes 153608 | tf_op jit(solution)/shard_map/ppermute | solution.py:19
  101.0 3.6 %collective-permute-start.11 = (f32[5,10,1,256]{3,0,2,1:T(8,128)S(1)}, f32[5,10,1,256]{3,0,2,1:T(8,128)S(1)}, u32[]{:S(2)}, u32[]{:S(2)}) collective-permute-start(f32[5,10,1,256]{3,0,2,1:T(8,128)S(1)} %get-tuple-element.8), channel_id=1, source_target_pairs={{0,1},{1,2},{2,3},{4,5},{5,6},{6,7},{8,9},{9,10},{10,11},{12,13},{... | collective-permute-start | bytes 153608 | tf_op jit(solution)/shard_map/ppermute | solution.py:16
  104.6 1.1 convolution_bitcast_fusion
  105.7 1.6 %collective-permute-done.11 = f32[5,10,1,256]{3,0,2,1:T(8,128)S(1)} collective-permute-done((f32[5,10,1,256]{3,0,2,1:T(8,128)S(1)}, f32[5,10,1,256]{3,0,2,1:T(8,128)S(1)}, u32[]{:S(2)}, u32[]{:S(2)}) %collective-permute-start.11) | collective-permute-done | bytes 51232 | tf_op jit(solution)/shard_map/ppermute | solution.py:16
  107.3 0.6 select_maximum_fusion
  108.0 1.0 convolution_bitcast_fusion.6
  109.0 1.2 %convolution_bitcast_fusion.7 = f32[5,8,16,256]{3,0,2,1:T(8,128)S(1)} fusion(f32[5,10,18,258]{3,0,2,1:T(8,128)S(1)} %select_maximum_fusion, f32[1,1,5,5]{3,2,1,0:T(8,128)S(1)} %copy.81), kind=kOutput, calls=%fused_computation.82 | convolution fusion | flops 9830400 | bytes 1708032 | tf_op jit(solution)/shard_map/ec,exyz->cxyz/dot_general | solution.py:34
  110.3 1.1 fusion.49
  111.3 1.1 fusion.52
  112.4 2.0 %fusion.86 = f32[1,5,8,16,256]{4,1,3,2,0:T(8,128)S(1)} fusion(f32[5,8,16,256]{3,0,2,1:T(8,128)S(1)} %convolution_bitcast_fusion.6, f32[5,8,16,256]{3,0,2,1:T(8,128)S(1)} %convolution_bitcast_fusion.7, f32[5,8,16,256]{3,0,2,1:T(8,128)S(1)} %fusion.49, f32[5,8,16,256]{3,0,2,1:T(8,128)S(1)} %fusion.52, f32[5,8,16,256]{3,0,2,1:T(8,128)S(1)} %convolution_bitcast_fusion, ...), kind=kOutput, calls=%fused_computation.100 | convolution fusion | flops 11325440 | bytes 5455972 | tf_op jit(solution)/shard_map/ec,exyz->cxyz/dot_general | solution.py:34
  114.4 1.0 copy.40
  (39 shorter events, 1.1 us)
Async XLA Ops:
  0.6 54.9 %copy-start = (f32[256,128]{1,0:T(8,128)S(1)}, f32[256,128]{1,0:T(8,128)}, u32[]{:S(2)}) copy-start(f32[256,128]{1,0:T(8,128)} %param.16) | copy-start | bytes 393220
  0.6 5.9 %copy-start.4 = (f32[1,6,5,5]{1,0,3,2:T(1,128)S(1)}, f32[1,6,5,5]{1,0,3,2:T(1,128)}, u32[]{:S(2)}) copy-start(f32[1,6,5,5]{1,0,3,2:T(1,128)} %param.12) | copy-start | bytes 1804
  0.7 6.9 %copy-start.6 = (s32[8,16]{1,0:T(8,128)S(1)}, s32[8,16]{1,0:T(8,128)}, u32[]{:S(2)}) copy-start(s32[8,16]{1,0:T(8,128)} %param.15) | copy-start | bytes 1540
  2.2 5.4 %collective-permute-start = (f32[5,1,16,256]{3,0,2,1:T(8,128)S(1)}, f32[5,1,16,256]{3,0,2,1:T(8,128)S(1)}, u32[]{:S(2)}, u32[]{:S(2)}) collective-permute-start(f32[5,1,16,256]{3,0,2,1:T(8,128)S(1)} %get-tuple-element.19), channel_id=1, source_target_pairs={{4,0},{8,4},{12,8},{5,1},{9,5},{13,9},{6,2},{10,6},{14,10},{7,3},{... | collective-permute-start | bytes 245768 | tf_op jit(solution)/shard_map/ppermute | solution.py:19
  4.1 6.3 %collective-permute-start.1 = (f32[5,1,16,256]{3,0,2,1:T(8,128)S(1)}, f32[5,1,16,256]{3,0,2,1:T(8,128)S(1)}, u32[]{:S(2)}, u32[]{:S(2)}) collective-permute-start(f32[5,1,16,256]{3,0,2,1:T(8,128)S(1)} %get-tuple-element.18), channel_id=1, source_target_pairs={{0,4},{4,8},{8,12},{1,5},{5,9},{9,13},{2,6},{6,10},{10,14},{3,7},{... | collective-permute-start | bytes 245768 | tf_op jit(solution)/shard_map/ppermute | solution.py:16
  10.4 6.9 %collective-permute-start.2 = (f32[5,10,1,256]{3,0,2,1:T(8,128)S(1)}, f32[5,10,1,256]{3,0,2,1:T(8,128)S(1)}, u32[]{:S(2)}, u32[]{:S(2)}) collective-permute-start(f32[5,10,1,256]{3,0,2,1:T(8,128)S(1)} %get-tuple-element.13), channel_id=1, source_target_pairs={{1,0},{2,1},{3,2},{5,4},{6,5},{7,6},{9,8},{10,9},{11,10},{13,12},{... | collective-permute-start | bytes 153608 | tf_op jit(solution)/shard_map/ppermute | solution.py:19
  12.8 6.3 %collective-permute-start.3 = (f32[5,10,1,256]{3,0,2,1:T(8,128)S(1)}, f32[5,10,1,256]{3,0,2,1:T(8,128)S(1)}, u32[]{:S(2)}, u32[]{:S(2)}) collective-permute-start(f32[5,10,1,256]{3,0,2,1:T(8,128)S(1)} %get-tuple-element.12), channel_id=1, source_target_pairs={{0,1},{1,2},{2,3},{4,5},{5,6},{6,7},{8,9},{9,10},{10,11},{12,13},{... | collective-permute-start | bytes 153608 | tf_op jit(solution)/shard_map/ppermute | solution.py:16
  22.1 2.2 %copy-start.1 = (f32[1,5,8,16,256]{4,3,2,1,0:T(8,128)S(1)}, f32[1,5,8,16,256]{4,3,2,1,0:T(8,128)}, u32[]{:S(2)}) copy-start(f32[1,5,8,16,256]{4,3,2,1,0:T(8,128)} %param.10) | copy-start | bytes 1966084
  22.1 2.2 %copy-start.2 = (f32[8,16,256]{2,1,0:T(8,128)S(1)}, f32[8,16,256]{2,1,0:T(8,128)}, u32[]{:S(2)}) copy-start(f32[8,16,256]{2,1,0:T(8,128)} %param.11) | copy-start | bytes 393220
  24.3 6.4 %copy-start.7 = (s32[2]{0:T(128)S(1)}, s32[2]{0:T(128)}, u32[]{:S(2)}) copy-start(s32[2]{0:T(128)} %param.17) | copy-start | bytes 28
  26.3 6.3 %collective-permute-start.4 = (f32[5,1,16,256]{3,0,2,1:T(8,128)S(1)}, f32[5,1,16,256]{3,0,2,1:T(8,128)S(1)}, u32[]{:S(2)}, u32[]{:S(2)}) collective-permute-start(f32[5,1,16,256]{3,0,2,1:T(8,128)S(1)} %get-tuple-element.17), channel_id=1, source_target_pairs={{4,0},{8,4},{12,8},{5,1},{9,5},{13,9},{6,2},{10,6},{14,10},{7,3},{... | collective-permute-start | bytes 245768 | tf_op jit(solution)/shard_map/ppermute | solution.py:19
  28.3 6.3 %collective-permute-start.5 = (f32[5,1,16,256]{3,0,2,1:T(8,128)S(1)}, f32[5,1,16,256]{3,0,2,1:T(8,128)S(1)}, u32[]{:S(2)}, u32[]{:S(2)}) collective-permute-start(f32[5,1,16,256]{3,0,2,1:T(8,128)S(1)} %get-tuple-element.16), channel_id=1, source_target_pairs={{0,4},{4,8},{8,12},{1,5},{5,9},{9,13},{2,6},{6,10},{10,14},{3,7},{... | collective-permute-start | bytes 245768 | tf_op jit(solution)/shard_map/ppermute | solution.py:16
  34.6 7.1 %collective-permute-start.6 = (f32[5,10,1,256]{3,0,2,1:T(8,128)S(1)}, f32[5,10,1,256]{3,0,2,1:T(8,128)S(1)}, u32[]{:S(2)}, u32[]{:S(2)}) collective-permute-start(f32[5,10,1,256]{3,0,2,1:T(8,128)S(1)} %get-tuple-element.11), channel_id=1, source_target_pairs={{1,0},{2,1},{3,2},{5,4},{6,5},{7,6},{9,8},{10,9},{11,10},{13,12},{... | collective-permute-start | bytes 153608 | tf_op jit(solution)/shard_map/ppermute | solution.py:19
  36.5 6.3 %collective-permute-start.7 = (f32[5,10,1,256]{3,0,2,1:T(8,128)S(1)}, f32[5,10,1,256]{3,0,2,1:T(8,128)S(1)}, u32[]{:S(2)}, u32[]{:S(2)}) collective-permute-start(f32[5,10,1,256]{3,0,2,1:T(8,128)S(1)} %get-tuple-element.10), channel_id=1, source_target_pairs={{0,1},{1,2},{2,3},{4,5},{5,6},{6,7},{8,9},{9,10},{10,11},{12,13},{... | collective-permute-start | bytes 153608 | tf_op jit(solution)/shard_map/ppermute | solution.py:16
  45.8 2.2 %copy-start.3 = (bf16[1,5,8,16,256]{4,3,2,1,0:T(8,128)(2,1)S(1)}, bf16[1,5,8,16,256]{4,3,2,1,0:T(8,128)(2,1)}, u32[]{:S(2)}) copy-start(bf16[1,5,8,16,256]{4,3,2,1,0:T(8,128)(2,1)} %param.13) | copy-start | bytes 983044
  50.1 5.4 %copy-start.5 = (s32[8,16,256]{2,1,0:T(8,128)S(1)}, s32[8,16,256]{2,1,0:T(8,128)}, u32[]{:S(2)}) copy-start(s32[8,16,256]{2,1,0:T(8,128)} %param.14) | copy-start | bytes 393220
  51.2 47.3 %collective-permute-start.8 = (f32[5,1,16,256]{3,0,2,1:T(8,128)S(1)}, f32[5,1,16,256]{3,0,2,1:T(8,128)S(1)}, u32[]{:S(2)}, u32[]{:S(2)}) collective-permute-start(f32[5,1,16,256]{3,0,2,1:T(8,128)S(1)} %get-tuple-element.15), channel_id=1, source_target_pairs={{4,0},{8,4},{12,8},{5,1},{9,5},{13,9},{6,2},{10,6},{14,10},{7,3},{... | collective-permute-start | bytes 245768 | tf_op jit(solution)/shard_map/ppermute | solution.py:19
  53.1 45.4 %collective-permute-start.9 = (f32[5,1,16,256]{3,0,2,1:T(8,128)S(1)}, f32[5,1,16,256]{3,0,2,1:T(8,128)S(1)}, u32[]{:S(2)}, u32[]{:S(2)}) collective-permute-start(f32[5,1,16,256]{3,0,2,1:T(8,128)S(1)} %get-tuple-element.14), channel_id=1, source_target_pairs={{0,4},{4,8},{8,12},{1,5},{5,9},{9,13},{2,6},{6,10},{10,14},{3,7},{... | collective-permute-start | bytes 245768 | tf_op jit(solution)/shard_map/ppermute | solution.py:16
  98.5 7.2 %collective-permute-start.10 = (f32[5,10,1,256]{3,0,2,1:T(8,128)S(1)}, f32[5,10,1,256]{3,0,2,1:T(8,128)S(1)}, u32[]{:S(2)}, u32[]{:S(2)}) collective-permute-start(f32[5,10,1,256]{3,0,2,1:T(8,128)S(1)} %get-tuple-element.9), channel_id=1, source_target_pairs={{1,0},{2,1},{3,2},{5,4},{6,5},{7,6},{9,8},{10,9},{11,10},{13,12},{... | collective-permute-start | bytes 153608 | tf_op jit(solution)/shard_map/ppermute | solution.py:19
  101.0 6.3 %collective-permute-start.11 = (f32[5,10,1,256]{3,0,2,1:T(8,128)S(1)}, f32[5,10,1,256]{3,0,2,1:T(8,128)S(1)}, u32[]{:S(2)}, u32[]{:S(2)}) collective-permute-start(f32[5,10,1,256]{3,0,2,1:T(8,128)S(1)} %get-tuple-element.8), channel_id=1, source_target_pairs={{0,1},{1,2},{2,3},{4,5},{5,6},{6,7},{8,9},{9,10},{10,11},{12,13},{... | collective-permute-start | bytes 153608 | tf_op jit(solution)/shard_map/ppermute | solution.py:16
where the time goes:
time: 116 us; the launch traced here: 115 us
  blocking collectives  41.7 us (36%)
  starting transfers between devices  30.9 us (27%)
  matrix products  23 us (20%)
  waiting for transfers between devices  9.19 us (8%)
  local copies, waits for them, and re-layouts  5.56 us (5%)
  other arithmetic  2.64 us (2%)
  between operations  2.47 us (2%)
    psum x1, blocking collectives, local(): summed = lax.psum(local_portion * gradient, ('cond', 'gx', 'yz'))  41.7 us
    dot_general x18, matrix products, apply_operator(): jnp.einsum('ec,exyz->cxyz', blocks[direction], shifted, precision=lax.Pre...  22.6 us
    ppermute x6, starting transfers between devices, with_halo(): lax.ppermute(lax.slice_in_dim(block, block.shape[dim] - width, None, axis...  18.4 us
    ppermute x6, starting transfers between devices, with_halo(): lax.ppermute(lax.slice_in_dim(block, 0, width, axis=dim), axis, backward)  12.5 us
    ppermute x6, waiting for transfers between devices, with_halo(): lax.ppermute(lax.slice_in_dim(block, block.shape[dim] - width, None, axis...  9.18 us
    unnamed x25, local copies, waits for them, and re-layouts  4.43 us
  transfers between devices with their start and end apart: 12, of which 5 were waited for; matrix products, arithmetic and copies ran while one was open for 5% of the time, Pallas kernels for 0%

commit v1 on v0

--- a/solution.py
+++ b/solution.py
@@ -91,7 +91,9 @@
     weights_float = condition_weights.astype(jnp.float32)
     picked = jnp.arange(weights_float.shape[0]) == lax.axis_index("cond")
     local_portion = jnp.sum(jnp.where(picked, weights_float, 0.0)) / jnp.sum(weights_float)
-    summed = lax.psum(local_portion * gradient, ("cond", "gx", "yz"))
+    summed = local_portion * gradient
+    for mesh_axis in (("gx", "yz"), "cond"):
+        summed = lax.psum(summed, mesh_axis)
     pieces = NDES // lax.axis_size(("gx", "yz"))
     design_gradient = lax.dynamic_slice_in_dim(
         summed, lax.axis_index(("gx", "yz")) * pieces, pieces, 0

time: 116 us -> 145 us (1.25)
  blocking collectives: 41.7 us -> 67.1 us
  starting transfers between devices: 30.9 us -> 33 us
  waiting for transfers between devices: 9.19 us -> 10.7 us
    psum x1 -> x2, blocking collectives: 41.7 us -> 67.1 us  [local(): summed = lax.psum(summed, mesh_axis)]
    ppermute x6, starting transfers between devices: 12.5 us -> 16 us  [with_halo(): lax.ppermute(lax.slice_in_dim(block, 0, width, axis=dim), axis, backward)]
    ppermute x6, starting transfers between devices: 18.4 us -> 17 us  [with_halo(): lax.ppermute(lax.slice_in_dim(block, block.shape[dim] - width, None, axis...]
    ppermute x6, waiting for transfers between devices: 9.18 us -> 10.7 us  [with_halo(): lax.ppermute(lax.slice_in_dim(block, block.shape[dim] - width, None, axis...]
  transfers between devices with their start and end apart: 12 -> 12, of which waited for: 5 -> 5; matrix products, arithmetic and copies ran while one was open for 5% -> 4% of each run, Pallas kernels for 0% -> 0%
where the time goes in v1:
time: 145 us; the launch traced here: 144 us
  blocking collectives  67.1 us (46%)
  starting transfers between devices  33 us (23%)
  matrix products  23 us (16%)
  waiting for transfers between devices  10.7 us (7%)
  local copies, waits for them, and re-layouts  5.55 us (4%)
  other arithmetic  2.64 us (2%)
  between operations  2.46 us (2%)
    psum x2, blocking collectives, local(): summed = lax.psum(summed, mesh_axis)  67.1 us
    dot_general x18, matrix products, apply_operator(): jnp.einsum('ec,exyz->cxyz', blocks[direction], shifted, precision=lax.Pre...  22.6 us
    ppermute x6, starting transfers between devices, with_halo(): lax.ppermute(lax.slice_in_dim(block, block.shape[dim] - width, None, axis...  17 us
    ppermute x6, starting transfers between devices, with_halo(): lax.ppermute(lax.slice_in_dim(block, 0, width, axis=dim), axis, backward)  16 us
    ppermute x6, waiting for transfers between devices, with_halo(): lax.ppermute(lax.slice_in_dim(block, block.shape[dim] - width, None, axis...  10.7 us
    unnamed x25, local copies, waits for them, and re-layouts  4.43 us
  transfers between devices with their start and end apart: 12, of which 5 were waited for; matrix products, arithmetic and copies ran while one was open for 4% of the time, Pallas kernels for 0%

profile of v1, /device:TPU:12, one launch (start us, length us, event | category | flops | bytes accessed | tf_op | source)
XLA Modules:
  0.0 144.4 jit_solution(2325376474875346467)
XLA Ops:
  0.7 1.5 %copy.88 = f32[1,5,8,16,256]{4,1,3,2,0:T(8,128)S(1)} copy(f32[1,5,8,16,256]{4,3,2,1,0:T(8,128)} %param.9) | data formatting | bytes 1310720 | tf_op args[0]
  2.2 1.9 %collective-permute-start = (f32[5,1,16,256]{3,0,2,1:T(8,128)S(1)}, f32[5,1,16,256]{3,0,2,1:T(8,128)S(1)}, u32[]{:S(2)}, u32[]{:S(2)}) collective-permute-start(f32[5,1,16,256]{3,0,2,1:T(8,128)S(1)} %get-tuple-element.19), channel_id=1, source_target_pairs={{4,0},{8,4},{12,8},{5,1},{9,5},{13,9},{6,2},{10,6},{14,10},{7,3},{... | collective-permute-start | bytes 245768 | tf_op jit(solution)/shard_map/ppermute | solution.py:19
  4.1 2.4 %collective-permute-start.1 = (f32[5,1,16,256]{3,0,2,1:T(8,128)S(1)}, f32[5,1,16,256]{3,0,2,1:T(8,128)S(1)}, u32[]{:S(2)}, u32[]{:S(2)}) collective-permute-start(f32[5,1,16,256]{3,0,2,1:T(8,128)S(1)} %get-tuple-element.18), channel_id=1, source_target_pairs={{0,4},{4,8},{8,12},{1,5},{5,9},{9,13},{2,6},{6,10},{10,14},{3,7},{... | collective-permute-start | bytes 245768 | tf_op jit(solution)/shard_map/ppermute | solution.py:16
  6.6 0.2 fusion.157
  7.7 2.8 %collective-permute-done.1 = f32[5,1,16,256]{3,0,2,1:T(8,128)S(1)} collective-permute-done((f32[5,1,16,256]{3,0,2,1:T(8,128)S(1)}, f32[5,1,16,256]{3,0,2,1:T(8,128)S(1)}, u32[]{:S(2)}, u32[]{:S(2)}) %collective-permute-start.1) | collective-permute-done | bytes 81952 | tf_op jit(solution)/shard_map/ppermute | solution.py:16
  10.4 2.4 %collective-permute-start.2 = (f32[5,10,1,256]{3,0,2,1:T(8,128)S(1)}, f32[5,10,1,256]{3,0,2,1:T(8,128)S(1)}, u32[]{:S(2)}, u32[]{:S(2)}) collective-permute-start(f32[5,10,1,256]{3,0,2,1:T(8,128)S(1)} %get-tuple-element.13), channel_id=1, source_target_pairs={{1,0},{2,1},{3,2},{5,4},{6,5},{7,6},{9,8},{10,9},{11,10},{13,12},{... | collective-permute-start | bytes 153608 | tf_op jit(solution)/shard_map/ppermute | solution.py:19
  12.8 3.5 %collective-permute-start.3 = (f32[5,10,1,256]{3,0,2,1:T(8,128)S(1)}, f32[5,10,1,256]{3,0,2,1:T(8,128)S(1)}, u32[]{:S(2)}, u32[]{:S(2)}) collective-permute-start(f32[5,10,1,256]{3,0,2,1:T(8,128)S(1)} %get-tuple-element.12), channel_id=1, source_target_pairs={{0,1},{1,2},{2,3},{4,5},{5,6},{6,7},{8,9},{9,10},{10,11},{12,13},{... | collective-permute-start | bytes 153608 | tf_op jit(solution)/shard_map/ppermute | solution.py:16
  16.3 1.1 convolution_bitcast_fusion.4
  17.4 1.8 %collective-permute-done.3 = f32[5,10,1,256]{3,0,2,1:T(8,128)S(1)} collective-permute-done((f32[5,10,1,256]{3,0,2,1:T(8,128)S(1)}, f32[5,10,1,256]{3,0,2,1:T(8,128)S(1)}, u32[]{:S(2)}, u32[]{:S(2)}) %collective-permute-start.3) | collective-permute-done | bytes 51232 | tf_op jit(solution)/shard_map/ppermute | solution.py:16
  19.1 0.6 select_maximum_fusion.8
  19.8 1.0 convolution_bitcast_fusion.10
  20.9 1.2 convolution_bitcast_fusion.11
  22.1 1.1 fusion.61
  23.2 1.1 fusion.64
  24.3 2.0 %fusion.94 = f32[5,8,16,256]{3,0,2,1:T(8,128)S(1)} fusion(f32[5,8,16,256]{3,0,2,1:T(8,128)S(1)} %bitcast.184, f32[5,8,16,256]{3,0,2,1:T(8,128)S(1)} %convolution_bitcast_fusion.10, f32[5,8,16,256]{3,0,2,1:T(8,128)S(1)} %convolution_bitcast_fusion.11, f32[5,8,16,256]{3,0,2,1:T(8,128)S(1)} %fusion.61, f32[5,8,16,256]{3,0,2,1:T(8,128)S(1)} %fusion.64, ...), kind=kOutput, calls=%fused_computation.108 | convolution fusion | flops 11816960 | bytes 5455972 | tf_op jit(solution)/shard_map/ec,exyz->cxyz/dot_general | solution.py:34
  26.3 1.9 %collective-permute-start.4 = (f32[5,1,16,256]{3,0,2,1:T(8,128)S(1)}, f32[5,1,16,256]{3,0,2,1:T(8,128)S(1)}, u32[]{:S(2)}, u32[]{:S(2)}) collective-permute-start(f32[5,1,16,256]{3,0,2,1:T(8,128)S(1)} %get-tuple-element.17), channel_id=1, source_target_pairs={{4,0},{8,4},{12,8},{5,1},{9,5},{13,9},{6,2},{10,6},{14,10},{7,3},{... | collective-permute-start | bytes 245768 | tf_op jit(solution)/shard_map/ppermute | solution.py:19
  28.3 2.4 %collective-permute-start.5 = (f32[5,1,16,256]{3,0,2,1:T(8,128)S(1)}, f32[5,1,16,256]{3,0,2,1:T(8,128)S(1)}, u32[]{:S(2)}, u32[]{:S(2)}) collective-permute-start(f32[5,1,16,256]{3,0,2,1:T(8,128)S(1)} %get-tuple-element.16), channel_id=1, source_target_pairs={{0,4},{4,8},{8,12},{1,5},{5,9},{9,13},{2,6},{6,10},{10,14},{3,7},{... | collective-permute-start | bytes 245768 | tf_op jit(solution)/shard_map/ppermute | solution.py:16
  30.7 0.6 convert_reduce_fusion
  32.7 1.9 %collective-permute-done.5 = f32[5,1,16,256]{3,0,2,1:T(8,128)S(1)} collective-permute-done((f32[5,1,16,256]{3,0,2,1:T(8,128)S(1)}, f32[5,1,16,256]{3,0,2,1:T(8,128)S(1)}, u32[]{:S(2)}, u32[]{:S(2)}) %collective-permute-start.5) | collective-permute-done | bytes 81952 | tf_op jit(solution)/shard_map/ppermute | solution.py:16
  34.6 1.9 %collective-permute-start.6 = (f32[5,10,1,256]{3,0,2,1:T(8,128)S(1)}, f32[5,10,1,256]{3,0,2,1:T(8,128)S(1)}, u32[]{:S(2)}, u32[]{:S(2)}) collective-permute-start(f32[5,10,1,256]{3,0,2,1:T(8,128)S(1)} %get-tuple-element.11), channel_id=1, source_target_pairs={{1,0},{2,1},{3,2},{5,4},{6,5},{7,6},{9,8},{10,9},{11,10},{13,12},{... | collective-permute-start | bytes 153608 | tf_op jit(solution)/shard_map/ppermute | solution.py:19
  36.5 4.1 %collective-permute-start.7 = (f32[5,10,1,256]{3,0,2,1:T(8,128)S(1)}, f32[5,10,1,256]{3,0,2,1:T(8,128)S(1)}, u32[]{:S(2)}, u32[]{:S(2)}) collective-permute-start(f32[5,10,1,256]{3,0,2,1:T(8,128)S(1)} %get-tuple-element.10), channel_id=1, source_target_pairs={{0,1},{1,2},{2,3},{4,5},{5,6},{6,7},{8,9},{9,10},{10,11},{12,13},{... | collective-permute-start | bytes 153608 | tf_op jit(solution)/shard_map/ppermute | solution.py:16
  40.6 1.1 convolution_bitcast_fusion.2
  41.7 1.1 collective-permute-done.7
  42.8 0.6 select_maximum_fusion.4
  43.5 1.0 convolution_bitcast_fusion.8
  44.5 1.2 convolution_bitcast_fusion.9
  45.8 1.1 fusion.55
  46.9 1.1 fusion.58
  47.9 2.2 %fusion.119 = (f32[8,16,256]{2,1,0:T(8,128)S(1)}, f32[5,8,16,256]{3,0,2,1:T(8,128)S(1)}) fusion(bf16[1,5,8,16,256]{4,3,2,1,0:T(8,128)(2,1)S(1)} %copy-done.3, f32[5,8,16,256]{3,0,2,1:T(8,128)S(1)} %fusion.94, f32[5,8,16,256]{3,0,2,1:T(8,128)S(1)} %convolution_bitcast_fusion.8, f32[5,8,16,256]{3,0,2,1:T(8,128)S(1)} %convolution_bitcast_fusion.9, ...), kind=kOutput, calls=%fused_computation.134 | convolution fusion | flops 12275712 | bytes 5914724 | tf_op jit(solution)/shard_map/ec,exyz->cxyz/dot_general | solution.py:34
  50.2 1.0 copy.39
  51.2 1.9 %collective-permute-start.8 = (f32[5,1,16,256]{3,0,2,1:T(8,128)S(1)}, f32[5,1,16,256]{3,0,2,1:T(8,128)S(1)}, u32[]{:S(2)}, u32[]{:S(2)}) collective-permute-start(f32[5,1,16,256]{3,0,2,1:T(8,128)S(1)} %get-tuple-element.15), channel_id=1, source_target_pairs={{4,0},{8,4},{12,8},{5,1},{9,5},{13,9},{6,2},{10,6},{14,10},{7,3},{... | collective-permute-start | bytes 245768 | tf_op jit(solution)/shard_map/ppermute | solution.py:19
  53.1 2.4 %collective-permute-start.9 = (f32[5,1,16,256]{3,0,2,1:T(8,128)S(1)}, f32[5,1,16,256]{3,0,2,1:T(8,128)S(1)}, u32[]{:S(2)}, u32[]{:S(2)}) collective-permute-start(f32[5,1,16,256]{3,0,2,1:T(8,128)S(1)} %get-tuple-element.14), channel_id=1, source_target_pairs={{0,4},{4,8},{8,12},{1,5},{5,9},{9,13},{2,6},{6,10},{10,14},{3,7},{... | collective-permute-start | bytes 245768 | tf_op jit(solution)/shard_map/ppermute | solution.py:16
  55.6 0.3 fusion.158
  55.8 0.2 fusion.120
  56.2 58.9 %psum.14 = f32[4096]{0:T(1024)S(1)} all-reduce(f32[4096]{0:T(1024)S(1)} %mul.57), channel_id=1, replica_groups=mesh['cond'=2,'gx'=4,'yz'=4] {'gx','yz'}, use_global_device_ids=true, to_apply=%region_3.4 | all-reduce | flops 4096 | bytes 32768 | tf_op jit(solution)/shard_map/psum | solution.py:96
  115.1 8.1 %psum.15 = f32[4096]{0:T(1024)S(1)} all-reduce(f32[4096]{0:T(1024)S(1)} %psum.14), channel_id=1, replica_groups=mesh['cond'=2,'gx'=4,'yz'=4] {'cond'}, use_global_device_ids=true, to_apply=%region_4.5 | all-reduce | flops 4096 | bytes 32768 | tf_op jit(solution)/shard_map/psum | solution.py:96
  123.3 0.6 dynamic_slice.3
  123.9 6.0 %collective-permute-start.10 = (f32[5,10,1,256]{3,0,2,1:T(8,128)S(1)}, f32[5,10,1,256]{3,0,2,1:T(8,128)S(1)}, u32[]{:S(2)}, u32[]{:S(2)}) collective-permute-start(f32[5,10,1,256]{3,0,2,1:T(8,128)S(1)} %get-tuple-element.9), channel_id=1, source_target_pairs={{1,0},{2,1},{3,2},{5,4},{6,5},{7,6},{9,8},{10,9},{11,10},{13,12},{... | collective-permute-start | bytes 153608 | tf_op jit(solution)/shard_map/ppermute | solution.py:19
  129.9 2.1 %collective-permute-start.11 = (f32[5,10,1,256]{3,0,2,1:T(8,128)S(1)}, f32[5,10,1,256]{3,0,2,1:T(8,128)S(1)}, u32[]{:S(2)}, u32[]{:S(2)}) collective-permute-start(f32[5,10,1,256]{3,0,2,1:T(8,128)S(1)} %get-tuple-element.8), channel_id=1, source_target_pairs={{0,1},{1,2},{2,3},{4,5},{5,6},{6,7},{8,9},{9,10},{10,11},{12,13},{... | collective-permute-start | bytes 153608 | tf_op jit(solution)/shard_map/ppermute | solution.py:16
  132.1 1.1 convolution_bitcast_fusion
  133.2 3.1 %collective-permute-done.11 = f32[5,10,1,256]{3,0,2,1:T(8,128)S(1)} collective-permute-done((f32[5,10,1,256]{3,0,2,1:T(8,128)S(1)}, f32[5,10,1,256]{3,0,2,1:T(8,128)S(1)}, u32[]{:S(2)}, u32[]{:S(2)}) %collective-permute-start.11) | collective-permute-done | bytes 51232 | tf_op jit(solution)/shard_map/ppermute | solution.py:16
  136.3 0.6 select_maximum_fusion
  136.9 1.0 convolution_bitcast_fusion.6
  138.0 1.2 convolution_bitcast_fusion.7
  139.2 1.1 fusion.49
  140.3 1.1 fusion.52
  141.4 2.0 %fusion.86 = f32[1,5,8,16,256]{4,1,3,2,0:T(8,128)S(1)} fusion(f32[5,8,16,256]{3,0,2,1:T(8,128)S(1)} %convolution_bitcast_fusion.6, f32[5,8,16,256]{3,0,2,1:T(8,128)S(1)} %convolution_bitcast_fusion.7, f32[5,8,16,256]{3,0,2,1:T(8,128)S(1)} %fusion.49, f32[5,8,16,256]{3,0,2,1:T(8,128)S(1)} %fusion.52, f32[5,8,16,256]{3,0,2,1:T(8,128)S(1)} %convolution_bitcast_fusion, ...), kind=kOutput, calls=%fused_computation.100 | convolution fusion | flops 11325440 | bytes 5455972 | tf_op jit(solution)/shard_map/ec,exyz->cxyz/dot_general | solution.py:34
  143.4 1.0 copy.40
  (40 shorter events, 1.2 us)
Async XLA Ops:
  0.6 54.9 %copy-start = (f32[256,128]{1,0:T(8,128)S(1)}, f32[256,128]{1,0:T(8,128)}, u32[]{:S(2)}) copy-start(f32[256,128]{1,0:T(8,128)} %param.16) | copy-start | bytes 393220
  0.6 5.9 %copy-start.4 = (f32[1,6,5,5]{1,0,3,2:T(1,128)S(1)}, f32[1,6,5,5]{1,0,3,2:T(1,128)}, u32[]{:S(2)}) copy-start(f32[1,6,5,5]{1,0,3,2:T(1,128)} %param.12) | copy-start | bytes 1804
  0.7 6.9 %copy-start.6 = (s32[8,16]{1,0:T(8,128)S(1)}, s32[8,16]{1,0:T(8,128)}, u32[]{:S(2)}) copy-start(s32[8,16]{1,0:T(8,128)} %param.15) | copy-start | bytes 1540
  2.2 5.4 %collective-permute-start = (f32[5,1,16,256]{3,0,2,1:T(8,128)S(1)}, f32[5,1,16,256]{3,0,2,1:T(8,128)S(1)}, u32[]{:S(2)}, u32[]{:S(2)}) collective-permute-start(f32[5,1,16,256]{3,0,2,1:T(8,128)S(1)} %get-tuple-element.19), channel_id=1, source_target_pairs={{4,0},{8,4},{12,8},{5,1},{9,5},{13,9},{6,2},{10,6},{14,10},{7,3},{... | collective-permute-start | bytes 245768 | tf_op jit(solution)/shard_map/ppermute | solution.py:19
  4.1 6.3 %collective-permute-start.1 = (f32[5,1,16,256]{3,0,2,1:T(8,128)S(1)}, f32[5,1,16,256]{3,0,2,1:T(8,128)S(1)}, u32[]{:S(2)}, u32[]{:S(2)}) collective-permute-start(f32[5,1,16,256]{3,0,2,1:T(8,128)S(1)} %get-tuple-element.18), channel_id=1, source_target_pairs={{0,4},{4,8},{8,12},{1,5},{5,9},{9,13},{2,6},{6,10},{10,14},{3,7},{... | collective-permute-start | bytes 245768 | tf_op jit(solution)/shard_map/ppermute | solution.py:16
  10.4 6.9 %collective-permute-start.2 = (f32[5,10,1,256]{3,0,2,1:T(8,128)S(1)}, f32[5,10,1,256]{3,0,2,1:T(8,128)S(1)}, u32[]{:S(2)}, u32[]{:S(2)}) collective-permute-start(f32[5,10,1,256]{3,0,2,1:T(8,128)S(1)} %get-tuple-element.13), channel_id=1, source_target_pairs={{1,0},{2,1},{3,2},{5,4},{6,5},{7,6},{9,8},{10,9},{11,10},{13,12},{... | collective-permute-start | bytes 153608 | tf_op jit(solution)/shard_map/ppermute | solution.py:19
  12.8 6.3 %collective-permute-start.3 = (f32[5,10,1,256]{3,0,2,1:T(8,128)S(1)}, f32[5,10,1,256]{3,0,2,1:T(8,128)S(1)}, u32[]{:S(2)}, u32[]{:S(2)}) collective-permute-start(f32[5,10,1,256]{3,0,2,1:T(8,128)S(1)} %get-tuple-element.12), channel_id=1, source_target_pairs={{0,1},{1,2},{2,3},{4,5},{5,6},{6,7},{8,9},{9,10},{10,11},{12,13},{... | collective-permute-start | bytes 153608 | tf_op jit(solution)/shard_map/ppermute | solution.py:16
  22.1 2.2 %copy-start.1 = (f32[1,5,8,16,256]{4,3,2,1,0:T(8,128)S(1)}, f32[1,5,8,16,256]{4,3,2,1,0:T(8,128)}, u32[]{:S(2)}) copy-start(f32[1,5,8,16,256]{4,3,2,1,0:T(8,128)} %param.10) | copy-start | bytes 1966084
  22.1 2.2 %copy-start.2 = (f32[8,16,256]{2,1,0:T(8,128)S(1)}, f32[8,16,256]{2,1,0:T(8,128)}, u32[]{:S(2)}) copy-start(f32[8,16,256]{2,1,0:T(8,128)} %param.11) | copy-start | bytes 393220
  24.3 6.4 %copy-start.7 = (s32[2]{0:T(128)S(1)}, s32[2]{0:T(128)}, u32[]{:S(2)}) copy-start(s32[2]{0:T(128)} %param.17) | copy-start | bytes 28
  26.3 6.3 %collective-permute-start.4 = (f32[5,1,16,256]{3,0,2,1:T(8,128)S(1)}, f32[5,1,16,256]{3,0,2,1:T(8,128)S(1)}, u32[]{:S(2)}, u32[]{:S(2)}) collective-permute-start(f32[5,1,16,256]{3,0,2,1:T(8,128)S(1)} %get-tuple-element.17), channel_id=1, source_target_pairs={{4,0},{8,4},{12,8},{5,1},{9,5},{13,9},{6,2},{10,6},{14,10},{7,3},{... | collective-permute-start | bytes 245768 | tf_op jit(solution)/shard_map/ppermute | solution.py:19
  28.3 6.3 %collective-permute-start.5 = (f32[5,1,16,256]{3,0,2,1:T(8,128)S(1)}, f32[5,1,16,256]{3,0,2,1:T(8,128)S(1)}, u32[]{:S(2)}, u32[]{:S(2)}) collective-permute-start(f32[5,1,16,256]{3,0,2,1:T(8,128)S(1)} %get-tuple-element.16), channel_id=1, source_target_pairs={{0,4},{4,8},{8,12},{1,5},{5,9},{9,13},{2,6},{6,10},{10,14},{3,7},{... | collective-permute-start | bytes 245768 | tf_op jit(solution)/shard_map/ppermute | solution.py:16
  34.6 7.1 %collective-permute-start.6 = (f32[5,10,1,256]{3,0,2,1:T(8,128)S(1)}, f32[5,10,1,256]{3,0,2,1:T(8,128)S(1)}, u32[]{:S(2)}, u32[]{:S(2)}) collective-permute-start(f32[5,10,1,256]{3,0,2,1:T(8,128)S(1)} %get-tuple-element.11), channel_id=1, source_target_pairs={{1,0},{2,1},{3,2},{5,4},{6,5},{7,6},{9,8},{10,9},{11,10},{13,12},{... | collective-permute-start | bytes 153608 | tf_op jit(solution)/shard_map/ppermute | solution.py:19
  36.5 6.3 %collective-permute-start.7 = (f32[5,10,1,256]{3,0,2,1:T(8,128)S(1)}, f32[5,10,1,256]{3,0,2,1:T(8,128)S(1)}, u32[]{:S(2)}, u32[]{:S(2)}) collective-permute-start(f32[5,10,1,256]{3,0,2,1:T(8,128)S(1)} %get-tuple-element.10), channel_id=1, source_target_pairs={{0,1},{1,2},{2,3},{4,5},{5,6},{6,7},{8,9},{9,10},{10,11},{12,13},{... | collective-permute-start | bytes 153608 | tf_op jit(solution)/shard_map/ppermute | solution.py:16
  45.8 2.2 %copy-start.3 = (bf16[1,5,8,16,256]{4,3,2,1,0:T(8,128)(2,1)S(1)}, bf16[1,5,8,16,256]{4,3,2,1,0:T(8,128)(2,1)}, u32[]{:S(2)}) copy-start(bf16[1,5,8,16,256]{4,3,2,1,0:T(8,128)(2,1)} %param.13) | copy-start | bytes 983044
  50.1 5.4 %copy-start.5 = (s32[8,16,256]{2,1,0:T(8,128)S(1)}, s32[8,16,256]{2,1,0:T(8,128)}, u32[]{:S(2)}) copy-start(s32[8,16,256]{2,1,0:T(8,128)} %param.14) | copy-start | bytes 393220
  51.2 72.7 %collective-permute-start.8 = (f32[5,1,16,256]{3,0,2,1:T(8,128)S(1)}, f32[5,1,16,256]{3,0,2,1:T(8,128)S(1)}, u32[]{:S(2)}, u32[]{:S(2)}) collective-permute-start(f32[5,1,16,256]{3,0,2,1:T(8,128)S(1)} %get-tuple-element.15), channel_id=1, source_target_pairs={{4,0},{8,4},{12,8},{5,1},{9,5},{13,9},{6,2},{10,6},{14,10},{7,3},{... | collective-permute-start | bytes 245768 | tf_op jit(solution)/shard_map/ppermute | solution.py:19
  53.1 70.8 %collective-permute-start.9 = (f32[5,1,16,256]{3,0,2,1:T(8,128)S(1)}, f32[5,1,16,256]{3,0,2,1:T(8,128)S(1)}, u32[]{:S(2)}, u32[]{:S(2)}) collective-permute-start(f32[5,1,16,256]{3,0,2,1:T(8,128)S(1)} %get-tuple-element.14), channel_id=1, source_target_pairs={{0,4},{4,8},{8,12},{1,5},{5,9},{9,13},{2,6},{6,10},{10,14},{3,7},{... | collective-permute-start | bytes 245768 | tf_op jit(solution)/shard_map/ppermute | solution.py:16
  123.9 9.3 %collective-permute-start.10 = (f32[5,10,1,256]{3,0,2,1:T(8,128)S(1)}, f32[5,10,1,256]{3,0,2,1:T(8,128)S(1)}, u32[]{:S(2)}, u32[]{:S(2)}) collective-permute-start(f32[5,10,1,256]{3,0,2,1:T(8,128)S(1)} %get-tuple-element.9), channel_id=1, source_target_pairs={{1,0},{2,1},{3,2},{5,4},{6,5},{7,6},{9,8},{10,9},{11,10},{13,12},{... | collective-permute-start | bytes 153608 | tf_op jit(solution)/shard_map/ppermute | solution.py:19
  129.9 6.3 %collective-permute-start.11 = (f32[5,10,1,256]{3,0,2,1:T(8,128)S(1)}, f32[5,10,1,256]{3,0,2,1:T(8,128)S(1)}, u32[]{:S(2)}, u32[]{:S(2)}) collective-permute-start(f32[5,10,1,256]{3,0,2,1:T(8,128)S(1)} %get-tuple-element.8), channel_id=1, source_target_pairs={{0,1},{1,2},{2,3},{4,5},{5,6},{6,7},{8,9},{9,10},{10,11},{12,13},{... | collective-permute-start | bytes 153608 | tf_op jit(solution)/shard_map/ppermute | solution.py:16
